TPU v7x, 32 devices: a whole 2x2x4 slice. The times are simulated.
32 devices in a mesh: rows: 4 (over y, core), cols: 4 (over z), heads: 2 (over x).
Axes of the slice: x: 2, y: 2, z: 4, core: 2. Of those that a mesh axis runs over, the one named last changes fastest.
Arguments:
- tokens: bfloat16 [16384, 1024], P(('rows', 'cols'), 'heads'), may hold values from -8 to 8
- ln_gain: float32 [1024], replicated, may hold values from 0.1 to 1.9
- w_qkv: bfloat16 [3, 1024, 1024], P(None, None, 'heads'), may hold values from -1 to 1
- w_out: bfloat16 [1024, 1024], P('heads'), may hold values from -0.1875 to 0.1875
- out_bias: float32 [1024], P('heads'), may hold values from -3 to 3
Outputs:
- mixed: bfloat16 [16384, 1024], P(('rows', 'cols'), 'heads')
All inputs are finite; a program needn't handle non-finite values.
Results may differ from a plain program's by a relative error of at most 0.0095.
Values may be sent and summed in bfloat16 or wider, within the bound.
A program may use at most 128 MiB of HBM per device.

v0:
```python
import jax
import jax.numpy as jnp
from jax import lax
from jax.sharding import PartitionSpec as P

D = 1024
HEADS = 16


def attend_keys(carry, keys, values, queries, scale):

    def one_block(args):
        rows, peak, total, accum = args
        scores = jnp.einsum("qhe,khe->hqk", rows, keys, preferred_element_type=jnp.float32) * scale
        newpeak = jnp.maximum(peak, jnp.max(scores, axis=-1))
        weights = jnp.exp(scores - newpeak[..., None])
        factor = jnp.exp(peak - newpeak)
        total = total * factor + jnp.sum(weights, axis=-1)
        accum = accum * factor[..., None] + jnp.einsum(
            "hqk,khe->hqe", weights.astype(jnp.bfloat16), values, preferred_element_type=jnp.float32
        )
        return (newpeak, total, accum)

    peak, total, accum = carry
    return lax.map(one_block, (queries, peak, total, accum))


def per_device(tokens, ln_gain, w_qkv, w_out, out_bias):
    whole = lax.all_gather(tokens, "heads", axis=1, tiled=True)
    xf = whole.astype(jnp.float32)
    mean = jnp.mean(xf, axis=-1, keepdims=True)
    centered = xf - mean
    var = jnp.mean(centered * centered, axis=-1, keepdims=True)
    normed = (centered * lax.rsqrt(var + 1e-06) * ln_gain).astype(jnp.bfloat16)
    projected = jnp.einsum("td,sde->ste", normed, w_qkv, preferred_element_type=jnp.float32).astype(
        jnp.bfloat16
    )
    head_dim = D // HEADS
    local_heads = w_out.shape[0] // head_dim
    tok_rows = tokens.shape[0]
    qblock = 512
    qcount = tok_rows // qblock
    scale = 1.0 / head_dim**0.5
    queries = projected[0].reshape(qcount, qblock, local_heads, head_dim)
    keys_local = projected[1]
    values_local = projected[2]
    initial = (
        jnp.full((qcount, local_heads, qblock), -jnp.inf, jnp.float32),
        jnp.zeros((qcount, local_heads, qblock), jnp.float32),
        jnp.zeros((qcount, local_heads, qblock, head_dim), jnp.float32),
    )
    keys = lax.all_gather(keys_local, ("rows", "cols"), axis=0, tiled=True)
    values = lax.all_gather(values_local, ("rows", "cols"), axis=0, tiled=True)
    count = keys.shape[0]
    kblock = 1024
    kblocks = keys.reshape(count // kblock, kblock, local_heads, head_dim)
    vblocks = values.reshape(count // kblock, kblock, local_heads, head_dim)

    def step(state, pair):
        return (attend_keys(state, pair[0], pair[1], queries, scale), None)

    result, unused = lax.scan(step, initial, (kblocks, vblocks))
    peak, total, accum = result
    attended = accum / total[..., None]
    attended = (
        attended.transpose(0, 2, 1, 3)
        .reshape(tok_rows, local_heads * head_dim)
        .astype(jnp.bfloat16)
    )
    partial_value = jnp.dot(attended, w_out, preferred_element_type=jnp.float32)
    summed = lax.psum_scatter(
        partial_value.astype(jnp.bfloat16), "heads", scatter_dimension=1, tiled=True
    ).astype(jnp.float32)
    return (tokens.astype(jnp.float32) + summed + out_bias).astype(jnp.bfloat16)


def solution(mesh):
    return jax.shard_map(
        per_device,
        mesh=mesh,
        in_specs=(
            P(("rows", "cols"), "heads"),
            P(),
            P(None, None, "heads"),
            P("heads", None),
            P("heads"),
        ),
        out_specs=P(("rows", "cols"), "heads"),
        check_vma=False,
    )
```

profile of v0, /device:TPU:0, one launch (start us, length us, event | category | flops | bytes accessed | tf_op | source)
XLA Modules:
  0.0 804.4 jit_solution(14423901690388378114)
XLA Ops:
  7.3 37.4 %all-gather.6.cloned.1.call-done = bf16[1024,1024]{1,0:T(8,128)(2,1)} async-done(((bf16[1024,512]{1,0:T(8,128)(2,1)}), bf16[1024,1024]{1,0:T(8,128)(2,1)}) %all-gather.6.cloned.1.call-update) | async-done | bytes 2097168 | tf_op jit(solution)/shard_map/all_gather | solution.py:29
  58.2 123.1 %all-gather.8.cloned.1.call-done = bf16[1,16384,512]{2,1,0:T(8,128)(2,1)} async-done(((bf16[1,1024,512]{2,1,0:T(8,128)(2,1)}), bf16[1,16384,512]{2,1,0:T(8,128)(2,1)}) %all-gather.8.cloned.1.call-update) | async-done | bytes 16777232 | tf_op jit(solution)/shard_map/all_gather | solution.py:52
  181.3 41.4 %reshape.50 = bf16[16,1024,8,64]{3,2,1,0:T(8,128)(2,1)} reshape(bf16[1,16384,512]{2,1,0:T(8,128)(2,1)} %all-gather.8.cloned.1.call-done) | data formatting | bytes 33554432 | tf_op jit(solution)/shard_map/reshape | solution.py:56
  222.7 35.9 %copy.12 = bf16[16,1024,8,64]{1,3,2,0:T(8,128)(2,1)} copy(bf16[16,1024,8,64]{3,2,1,0:T(8,128)(2,1)} %reshape.50) | data formatting | bytes 33554432 | tf_op jit(solution)/shard_map/while | solution.py:62
  258.6 49.6 %all-gather.10.cloned.1.call-done = bf16[1,16384,512]{2,1,0:T(8,128)(2,1)} async-done(((bf16[1,1024,512]{2,1,0:T(8,128)(2,1)}), bf16[1,16384,512]{2,1,0:T(8,128)(2,1)}) %all-gather.10.cloned.1.call-update) | async-done | bytes 16777232 | tf_op jit(solution)/shard_map/all_gather | solution.py:53
  308.1 41.3 %reshape.51 = bf16[16,1024,8,64]{3,2,1,0:T(8,128)(2,1)} reshape(bf16[1,16384,512]{2,1,0:T(8,128)(2,1)} %all-gather.10.cloned.1.call-done) | data formatting | bytes 33554432 | tf_op jit(solution)/shard_map/reshape | solution.py:57
  349.5 35.4 %copy.13 = bf16[16,1024,8,64]{1,3,2,0:T(8,128)(2,1)} copy(bf16[16,1024,8,64]{3,2,1,0:T(8,128)(2,1)} %reshape.51) | data formatting | bytes 33554432 | tf_op jit(solution)/shard_map/while | solution.py:62
  386.5 372.3 %while.30 = (s32[]{:T(128)}, f32[2,8,512]{2,1,0:T(8,128)S(1)}, f32[2,8,512]{2,1,0:T(8,128)S(1)}, f32[2,8,512,64]{2,3,1,0:T(8,128)}, bf16[16,1024,8,64]{1,3,2,0:T...) while((s32[]{:T(128)}, f32[2,8,512]{2,1,0:T(8,128)S(1)}, ...), condition=%wide.region_7.8_spmd, body=%wide.region_2.7_spmd.sunk | while | flops 1107836928 | bytes 86753680 | solution.py:62
  388.3 21.5 %while.31 = (s32[]{:T(128)}, f32[2,8,512]{2,1,0:T(8,128)S(1)}, f32[2,8,512]{2,1,0:T(8,128)S(1)}, f32[2,8,512,64]{2,3,1,0:T(8,128)}, bf16[2,512,8,64]{1,3,2,0:T(8...) while((s32[]{:T(128)}, f32[2,8,512]{2,1,0:T(8,128)S(1)}, ...), condition=%wide.region_6.6_spmd.clone, body=%wide.region_3.5_spmd.clone.sunk | while | flops 1107836928 | bytes 82559200 | solution.py:25
  390.9 4.5 fusion.51
  401.7 4.5 fusion.51
  411.5 21.5 %while.31 = (s32[]{:T(128)}, f32[2,8,512]{2,1,0:T(8,128)S(1)}, f32[2,8,512]{2,1,0:T(8,128)S(1)}, f32[2,8,512,64]{2,3,1,0:T(8,128)}, bf16[2,512,8,64]{1,3,2,0:T(8...) while((s32[]{:T(128)}, f32[2,8,512]{2,1,0:T(8,128)S(1)}, ...), condition=%wide.region_6.6_spmd.clone, body=%wide.region_3.5_spmd.clone.sunk | while | flops 1107836928 | bytes 82559200 | solution.py:25
  414.2 4.5 fusion.51
  424.9 4.5 fusion.51
  434.8 21.5 %while.31 = (s32[]{:T(128)}, f32[2,8,512]{2,1,0:T(8,128)S(1)}, f32[2,8,512]{2,1,0:T(8,128)S(1)}, f32[2,8,512,64]{2,3,1,0:T(8,128)}, bf16[2,512,8,64]{1,3,2,0:T(8...) while((s32[]{:T(128)}, f32[2,8,512]{2,1,0:T(8,128)S(1)}, ...), condition=%wide.region_6.6_spmd.clone, body=%wide.region_3.5_spmd.clone.sunk | while | flops 1107836928 | bytes 82559200 | solution.py:25
  437.5 4.5 fusion.51
  458.1 21.5 %while.31 = (s32[]{:T(128)}, f32[2,8,512]{2,1,0:T(8,128)S(1)}, f32[2,8,512]{2,1,0:T(8,128)S(1)}, f32[2,8,512,64]{2,3,1,0:T(8,128)}, bf16[2,512,8,64]{1,3,2,0:T(8...) while((s32[]{:T(128)}, f32[2,8,512]{2,1,0:T(8,128)S(1)}, ...), condition=%wide.region_6.6_spmd.clone, body=%wide.region_3.5_spmd.clone.sunk | while | flops 1107836928 | bytes 82559200 | solution.py:25
  460.7 4.5 fusion.51
  471.5 4.5 fusion.51
  481.3 21.5 %while.31 = (s32[]{:T(128)}, f32[2,8,512]{2,1,0:T(8,128)S(1)}, f32[2,8,512]{2,1,0:T(8,128)S(1)}, f32[2,8,512,64]{2,3,1,0:T(8,128)}, bf16[2,512,8,64]{1,3,2,0:T(8...) while((s32[]{:T(128)}, f32[2,8,512]{2,1,0:T(8,128)S(1)}, ...), condition=%wide.region_6.6_spmd.clone, body=%wide.region_3.5_spmd.clone.sunk | while | flops 1107836928 | bytes 82559200 | solution.py:25
  484.0 4.5 fusion.51
  504.6 21.5 %while.31 = (s32[]{:T(128)}, f32[2,8,512]{2,1,0:T(8,128)S(1)}, f32[2,8,512]{2,1,0:T(8,128)S(1)}, f32[2,8,512,64]{2,3,1,0:T(8,128)}, bf16[2,512,8,64]{1,3,2,0:T(8...) while((s32[]{:T(128)}, f32[2,8,512]{2,1,0:T(8,128)S(1)}, ...), condition=%wide.region_6.6_spmd.clone, body=%wide.region_3.5_spmd.clone.sunk | while | flops 1107836928 | bytes 82559200 | solution.py:25
  507.3 4.5 fusion.51
  518.0 4.5 fusion.51
  527.9 21.5 %while.31 = (s32[]{:T(128)}, f32[2,8,512]{2,1,0:T(8,128)S(1)}, f32[2,8,512]{2,1,0:T(8,128)S(1)}, f32[2,8,512,64]{2,3,1,0:T(8,128)}, bf16[2,512,8,64]{1,3,2,0:T(8...) while((s32[]{:T(128)}, f32[2,8,512]{2,1,0:T(8,128)S(1)}, ...), condition=%wide.region_6.6_spmd.clone, body=%wide.region_3.5_spmd.clone.sunk | while | flops 1107836928 | bytes 82559200 | solution.py:25
  530.5 4.5 fusion.51
  541.3 4.5 fusion.51
  551.2 21.5 %while.31 = (s32[]{:T(128)}, f32[2,8,512]{2,1,0:T(8,128)S(1)}, f32[2,8,512]{2,1,0:T(8,128)S(1)}, f32[2,8,512,64]{2,3,1,0:T(8,128)}, bf16[2,512,8,64]{1,3,2,0:T(8...) while((s32[]{:T(128)}, f32[2,8,512]{2,1,0:T(8,128)S(1)}, ...), condition=%wide.region_6.6_spmd.clone, body=%wide.region_3.5_spmd.clone.sunk | while | flops 1107836928 | bytes 82559200 | solution.py:25
  564.5 4.5 fusion.51
  574.4 21.5 %while.31 = (s32[]{:T(128)}, f32[2,8,512]{2,1,0:T(8,128)S(1)}, f32[2,8,512]{2,1,0:T(8,128)S(1)}, f32[2,8,512,64]{2,3,1,0:T(8,128)}, bf16[2,512,8,64]{1,3,2,0:T(8...) while((s32[]{:T(128)}, f32[2,8,512]{2,1,0:T(8,128)S(1)}, ...), condition=%wide.region_6.6_spmd.clone, body=%wide.region_3.5_spmd.clone.sunk | while | flops 1107836928 | bytes 82559200 | solution.py:25
  587.8 4.5 fusion.51
  597.7 21.5 %while.31 = (s32[]{:T(128)}, f32[2,8,512]{2,1,0:T(8,128)S(1)}, f32[2,8,512]{2,1,0:T(8,128)S(1)}, f32[2,8,512,64]{2,3,1,0:T(8,128)}, bf16[2,512,8,64]{1,3,2,0:T(8...) while((s32[]{:T(128)}, f32[2,8,512]{2,1,0:T(8,128)S(1)}, ...), condition=%wide.region_6.6_spmd.clone, body=%wide.region_3.5_spmd.clone.sunk | while | flops 1107836928 | bytes 82559200 | solution.py:25
  600.4 4.5 fusion.51
  611.1 4.5 fusion.51
  621.0 21.5 %while.31 = (s32[]{:T(128)}, f32[2,8,512]{2,1,0:T(8,128)S(1)}, f32[2,8,512]{2,1,0:T(8,128)S(1)}, f32[2,8,512,64]{2,3,1,0:T(8,128)}, bf16[2,512,8,64]{1,3,2,0:T(8...) while((s32[]{:T(128)}, f32[2,8,512]{2,1,0:T(8,128)S(1)}, ...), condition=%wide.region_6.6_spmd.clone, body=%wide.region_3.5_spmd.clone.sunk | while | flops 1107836928 | bytes 82559200 | solution.py:25
  623.6 4.5 fusion.51
  644.2 21.5 %while.31 = (s32[]{:T(128)}, f32[2,8,512]{2,1,0:T(8,128)S(1)}, f32[2,8,512]{2,1,0:T(8,128)S(1)}, f32[2,8,512,64]{2,3,1,0:T(8,128)}, bf16[2,512,8,64]{1,3,2,0:T(8...) while((s32[]{:T(128)}, f32[2,8,512]{2,1,0:T(8,128)S(1)}, ...), condition=%wide.region_6.6_spmd.clone, body=%wide.region_3.5_spmd.clone.sunk | while | flops 1107836928 | bytes 82559200 | solution.py:25
  646.9 4.5 fusion.51
  667.5 21.5 %while.31 = (s32[]{:T(128)}, f32[2,8,512]{2,1,0:T(8,128)S(1)}, f32[2,8,512]{2,1,0:T(8,128)S(1)}, f32[2,8,512,64]{2,3,1,0:T(8,128)}, bf16[2,512,8,64]{1,3,2,0:T(8...) while((s32[]{:T(128)}, f32[2,8,512]{2,1,0:T(8,128)S(1)}, ...), condition=%wide.region_6.6_spmd.clone, body=%wide.region_3.5_spmd.clone.sunk | while | flops 1107836928 | bytes 82559200 | solution.py:25
  670.2 4.5 fusion.51
  690.8 21.5 %while.31 = (s32[]{:T(128)}, f32[2,8,512]{2,1,0:T(8,128)S(1)}, f32[2,8,512]{2,1,0:T(8,128)S(1)}, f32[2,8,512,64]{2,3,1,0:T(8,128)}, bf16[2,512,8,64]{1,3,2,0:T(8...) while((s32[]{:T(128)}, f32[2,8,512]{2,1,0:T(8,128)S(1)}, ...), condition=%wide.region_6.6_spmd.clone, body=%wide.region_3.5_spmd.clone.sunk | while | flops 1107836928 | bytes 82559200 | solution.py:25
  693.4 4.5 fusion.51
  714.0 21.5 %while.31 = (s32[]{:T(128)}, f32[2,8,512]{2,1,0:T(8,128)S(1)}, f32[2,8,512]{2,1,0:T(8,128)S(1)}, f32[2,8,512,64]{2,3,1,0:T(8,128)}, bf16[2,512,8,64]{1,3,2,0:T(8...) while((s32[]{:T(128)}, f32[2,8,512]{2,1,0:T(8,128)S(1)}, ...), condition=%wide.region_6.6_spmd.clone, body=%wide.region_3.5_spmd.clone.sunk | while | flops 1107836928 | bytes 82559200 | solution.py:25
  716.7 4.5 fusion.51
  727.4 4.5 fusion.51
  737.3 21.5 %while.31 = (s32[]{:T(128)}, f32[2,8,512]{2,1,0:T(8,128)S(1)}, f32[2,8,512]{2,1,0:T(8,128)S(1)}, f32[2,8,512,64]{2,3,1,0:T(8,128)}, bf16[2,512,8,64]{1,3,2,0:T(8...) while((s32[]{:T(128)}, f32[2,8,512]{2,1,0:T(8,128)S(1)}, ...), condition=%wide.region_6.6_spmd.clone, body=%wide.region_3.5_spmd.clone.sunk | while | flops 1107836928 | bytes 82559200 | solution.py:25
  740.0 4.5 fusion.51
  764.8 30.2 %reduce-scatter.2.cloned.1.call-done = bf16[1024,512]{1,0:T(8,128)(2,1)} async-done(((bf16[1024,1024]{1,0:T(8,128)(2,1)}), bf16[1024,512]{1,0:T(8,128)(2,1)}) %reduce-scatter.2.cloned.1.call-update) | async-done | bytes 1048592 | tf_op jit(solution)/shard_map/reduce_scatter | solution.py:71
  (477 shorter events, 288.5 us)
Async XLA Ops:
  6.5 42.6 %copy-start = (bf16[3,1024,512]{2,1,0:T(8,128)(2,1)S(1)}, bf16[3,1024,512]{2,1,0:T(8,128)(2,1)}, u32[]{:S(2)}) copy-start(bf16[3,1024,512]{2,1,0:T(8,128)(2,1)} %param.11) | copy-start | bytes 9437188
  6.5 42.6 %copy-start.9 = (f32[1024]{0:T(1024)S(1)}, f32[1024]{0:T(1024)}, u32[]{:S(2)}) copy-start(f32[1024]{0:T(1024)} %param.10) | copy-start | bytes 12292
  6.5 38.2 %all-gather.6.cloned.1.call-start = ((), (), s32[]{:S(2)}) async-start(), calls=%async_computation.1 | async-start | bytes 3145728 | tf_op jit(solution)/shard_map/all_gather | solution.py:29
  7.3 174.0 %all-gather.8.cloned.1.call-start = ((), (), s32[]{:S(2)}) async-start(), calls=%async_computation.3 | async-start | bytes 17825792 | tf_op jit(solution)/shard_map/all_gather | solution.py:52
  44.7 4.4 copy-start.6
  54.7 253.4 %all-gather.10.cloned.1.call-start = ((), (), s32[]{:S(2)}) async-start(), calls=%async_computation.4 | async-start | bytes 17825792 | tf_op jit(solution)/shard_map/all_gather | solution.py:53
  55.5 739.6 %reduce-scatter.2.cloned.1.call-start = ((), (), s32[]{:S(2)}) async-start(), calls=%async_computation.2 | async-start | bytes 3145728 | tf_op jit(solution)/shard_map/reduce_scatter | solution.py:71
  395.5 3.5 copy-start.3
  395.5 3.5 copy-start.5
  406.2 3.5 copy-start.3
  406.2 3.5 copy-start.5
  418.7 3.5 copy-start.3
  418.7 3.5 copy-start.5
  429.5 3.5 copy-start.3
  429.5 3.5 copy-start.5
  442.0 3.5 copy-start.3
  442.0 3.5 copy-start.5
  452.7 3.5 copy-start.3
  452.7 3.5 copy-start.5
  465.3 3.5 copy-start.3
  465.3 3.5 copy-start.5
  476.0 3.5 copy-start.5
  488.5 3.5 copy-start.5
  499.3 3.5 copy-start.5
  511.8 3.5 copy-start.5
  522.5 3.5 copy-start.5
  535.1 3.5 copy-start.5
  545.8 3.5 copy-start.5
  558.4 3.5 copy-start.5
  569.1 3.5 copy-start.5
  581.6 3.5 copy-start.5
  592.4 3.5 copy-start.5
  604.9 3.5 copy-start.5
  615.7 3.5 copy-start.5
  628.2 3.5 copy-start.5
  638.9 3.5 copy-start.5
  651.5 3.5 copy-start.5
  662.2 3.5 copy-start.5
  674.7 3.5 copy-start.5
  685.5 3.5 copy-start.5
  698.0 3.5 copy-start.5
  708.7 3.5 copy-start.5
  721.3 3.5 copy-start.5
  732.0 3.5 copy-start.5
  744.5 3.5 copy-start.5
  755.3 3.5 copy-start.5
  762.1 32.9 %copy-start.7 = (f32[512]{0:T(512)S(1)}, f32[512]{0:T(512)}, u32[]{:S(2)}) copy-start(f32[512]{0:T(512)} %param.13) | copy-start | bytes 6148
  762.1 35.7 %copy-start.1 = (bf16[3,1024,512]{2,1,0:T(8,128)(2,1)S(1)}, bf16[3,1024,512]{2,1,0:T(8,128)(2,1)}, u32[]{:S(2)}) copy-start(bf16[3,1024,512]{2,1,0:T(8,128)(2,1)} %param.11) | copy-start | bytes 9437188
  (90 other events, 250.4 us)
Sparse Core Ops, SparseCore 0:
  8.9 35.8 all-gather.5
  54.8 126.4 all-gather.7
  183.5 124.5 all-gather.9
  764.9 30.0 reduce-scatter.1
where the time goes:
time: 809 us; the launch traced here: 804 us
  waiting for transfers between devices  242 us (30%)
  matrix products  231 us (29%)
  local copies, waits for them, and re-layouts  194 us (24%)
  other arithmetic  121 us (15%)
  between operations  13.3 us (2%)
    dot_general x32, matrix products, one_block(): jnp.einsum('hqk,khe->hqe', weights.astype(jnp.bfloat16), values, preferre...  145 us
    all_gather x1, waiting for transfers between devices, per_device(): keys = lax.all_gather(keys_local, ('rows', 'cols'), axis=0, tiled=True)  123 us
    reduce_sum x32, other arithmetic, one_block(): total = total * factor + jnp.sum(weights, axis=-1)  110 us
    dot_general x32, matrix products, one_block(): jnp.einsum('qhe,khe->hqk', rows, keys, preferred_element_type=jnp.float32)  78.9 us
    while x3, local copies, waits for them, and re-layouts, per_device(): result, unused = lax.scan(step, initial, (kblocks, vblocks))  72.7 us
    all_gather x1, waiting for transfers between devices, per_device(): values = lax.all_gather(values_local, ('rows', 'cols'), axis=0, tiled=True)  49.6 us
    reshape x1, local copies, waits for them, and re-layouts, per_device(): kblocks = keys.reshape(count // kblock, kblock, local_heads, head_dim)  41.4 us
    reshape x1, local copies, waits for them, and re-layouts, per_device(): vblocks = values.reshape(count // kblock, kblock, local_heads, head_dim)  41.3 us
  transfers between devices with their start and end apart: 4, of which 4 were waited for; matrix products, arithmetic and copies ran while one was open for 10% of the time, Pallas kernels for 0%

commit v1 on v0

v1 whole, which is shorter than its diff:
```python
import functools
import math

import jax
import jax.numpy as jnp
from jax import lax
from jax.experimental import pallas as pl
from jax.experimental.pallas import tpu as pltpu
from jax.sharding import PartitionSpec as P

D = 1024
HEADS = 16
HEAD_DIM = D // HEADS
PAIR = 2 * HEAD_DIM
EXTRA = 16
QB = 256
SAFE = 100.0


def attend_kernel(first, last, info_ref, q_ref, k_ref, v_ref, *rest):
    if not first:
        acc_in, peak_in = rest[:2]
        rest = rest[2:]
    if last:
        out_ref, acc_ref, peak_ref = rest
    else:
        acc_ref, peak_ref = rest
    step = pl.program_id(1)
    heads = q_ref.shape[0]
    rows = v_ref.shape[1] // heads
    kb = k_ref.shape[1]
    qn = q_ref.shape[2]
    qb = min(QB, qn)

    @pl.when(step == 0)
    def _():
        if first:
            acc_ref[...] = jnp.zeros_like(acc_ref)
            peak_ref[...] = jnp.full_like(peak_ref, -jnp.inf)
        else:
            acc_ref[...] = acc_in[...]
            peak_ref[...] = peak_in[...]

    def scores(h, j):
        return jnp.dot(
            k_ref[0], q_ref[h, :, j * qb : (j + 1) * qb], preferred_element_type=jnp.float32
        )

    def weigh(h, probs):
        ones = jnp.ones((EXTRA, kb), jnp.bfloat16)
        lhs = jnp.concatenate([v_ref[0, h * rows : (h + 1) * rows, :], ones], axis=0)
        return jnp.dot(lhs, probs, preferred_element_type=jnp.float32)

    units = [(h, j) for h in range(heads) for j in range(qn // qb)]

    @pl.when(info_ref[1] == 1)
    def _():
        def body(j, carry):
            cols = pl.ds(pl.multiple_of(j * qb, qb), qb)
            all_s = [
                jnp.dot(k_ref[0], q_ref[h, :, cols], preferred_element_type=jnp.float32)
                for h in range(heads)
            ]
            for h in range(heads):
                acc_ref[h, :, cols] += weigh(h, jnp.exp2(all_s[h]).astype(jnp.bfloat16))
            return carry

        lax.fori_loop(0, qn // qb, body, 0, unroll=2)

    @pl.when(info_ref[1] != 1)
    def _():
        for h in range(heads):

            def body(j, carry):
                cols = pl.ds(pl.multiple_of(j * qb, qb), qb)
                s = jnp.dot(k_ref[0], q_ref[h, :, cols], preferred_element_type=jnp.float32)
                old = jnp.max(peak_ref[h, :, cols], axis=0, keepdims=True)
                new = jnp.maximum(old, jnp.max(s, axis=0, keepdims=True))
                probs = jnp.exp2(s - new).astype(jnp.bfloat16)
                acc_ref[h, :, cols] = acc_ref[h, :, cols] * jnp.exp2(old - new) + weigh(h, probs)
                peak_ref[h, :, cols] = jnp.broadcast_to(new, (8, qb))
                return carry

            lax.fori_loop(0, qn // qb, body, 0)

    if last:

        @pl.when(step == pl.num_programs(1) - 1)
        def _():
            for h in range(heads):
                den = jnp.max(acc_ref[h, rows:, :], axis=0, keepdims=True)
                out_ref[h * rows : (h + 1) * rows, :] = (acc_ref[h, :rows, :] / den).astype(jnp.bfloat16)


def attend(info, queries, keys, values, state, first, last, name):
    heads, width, qn = queries.shape
    groups, kb, lanes = keys.shape
    pairs = lanes // PAIR
    steps = groups if first else groups - 1
    tall = HEAD_DIM + EXTRA

    def tile(p, g, info):
        if first:
            return g
        return lax.rem(info[0] + 1 + g, groups)

    in_specs = [
        pl.BlockSpec((2, width, qn), lambda p, g, info: (p, 0, 0)),
        pl.BlockSpec((1, kb, PAIR), lambda p, g, info: (tile(p, g, info), 0, p)),
        pl.BlockSpec((1, PAIR, kb), lambda p, g, info: (tile(p, g, info), p, 0)),
    ]
    state_specs = [
        pl.BlockSpec((2, tall, qn), lambda p, g, info: (p, 0, 0)),
        pl.BlockSpec((2, 8, qn), lambda p, g, info: (p, 0, 0)),
    ]
    state_shapes = [
        jax.ShapeDtypeStruct((heads, tall, qn), jnp.float32),
        jax.ShapeDtypeStruct((heads, 8, qn), jnp.float32),
    ]
    out_specs, out_shape, scratch = state_specs, state_shapes, []
    if last:
        out_specs = [pl.BlockSpec((PAIR, qn), lambda p, g, info: (p, 0))]
        out_shape = [jax.ShapeDtypeStruct((heads * HEAD_DIM, qn), jnp.bfloat16)]
        scratch = [pltpu.VMEM((2, tall, qn), jnp.float32), pltpu.VMEM((2, 8, qn), jnp.float32)]
    args = [queries, keys, values]
    if not first:
        in_specs = in_specs + state_specs
        args += list(state)
    work = heads * steps * kb * qn
    return pl.pallas_call(
        functools.partial(attend_kernel, first, last),
        grid_spec=pltpu.PrefetchScalarGridSpec(
            num_scalar_prefetch=1,
            grid=(pairs, steps),
            in_specs=in_specs,
            out_specs=out_specs,
            scratch_shapes=scratch,
        ),
        out_shape=out_shape,
        compiler_params=pltpu.CompilerParams(
            dimension_semantics=("arbitrary", "arbitrary"), vmem_limit_bytes=48 * 1024 * 1024
        ),
        cost_estimate=pl.CostEstimate(
            flops=16 * HEAD_DIM * work, bytes_accessed=4 * steps * kb * lanes, transcendentals=work
        ),
        name=name,
    )(info, *args)


def per_device(cuts, tokens, ln_gain, w_qkv, w_out, out_bias):
    whole = lax.all_gather(tokens, "heads", axis=1, tiled=True)
    xf = whole.astype(jnp.float32)
    mean = jnp.mean(xf, axis=-1, keepdims=True)
    centered = xf - mean
    var = jnp.mean(centered * centered, axis=-1, keepdims=True)
    normed = (centered * lax.rsqrt(var + 1e-06) * ln_gain).astype(jnp.bfloat16)

    both = ("rows", "cols")
    tok = tokens.shape[0]
    heads = w_out.shape[0] // HEAD_DIM
    keys = jnp.dot(normed, w_qkv[1], preferred_element_type=jnp.float32).astype(jnp.bfloat16)
    values = lax.dot_general(
        w_qkv[2], normed, (((0,), (1,)), ((), ())), preferred_element_type=jnp.float32
    ).astype(jnp.bfloat16)
    edges = [sum(cuts[:i]) * tok // sum(cuts) for i in range(len(cuts) + 1)]
    gathered = []
    for lo, hi in zip(edges[:-1], edges[1:]):
        kg = lax.all_gather(keys[lo:hi], both, axis=0)
        vg = lax.all_gather(values[:, lo:hi], both, axis=0)
        gathered.append((kg, vg))

    factor = math.log2(math.e) / HEAD_DIM**0.5
    queries = (
        lax.dot_general(
            w_qkv[0], normed, (((0,), (1,)), ((), ())), preferred_element_type=jnp.float32
        )
        * factor
    ).astype(jnp.bfloat16)
    byhead = queries.reshape(heads // 2, 2, 1, HEAD_DIM, tok)
    own = jnp.eye(2, dtype=jnp.bfloat16).reshape(1, 2, 2, 1, 1)
    padded = (byhead * own).reshape(heads, PAIR, tok)

    member = jnp.repeat(jnp.eye(heads, dtype=jnp.bfloat16), HEAD_DIM, axis=0)
    ksquare = jnp.square(keys.astype(jnp.float32)).astype(jnp.bfloat16)
    knorm = jnp.max(jnp.dot(ksquare, member, preferred_element_type=jnp.float32), axis=0)
    knorm = lax.pmax(knorm, both)
    qsquare = jnp.square(queries.astype(jnp.float32)).astype(jnp.bfloat16)
    qnorm = jnp.max(jnp.dot(member.T, qsquare, preferred_element_type=jnp.float32), axis=1)
    safe = jnp.all(knorm * qnorm <= SAFE * SAFE)
    info = jnp.stack([lax.axis_index(both).astype(jnp.int32), safe.astype(jnp.int32)])

    state = attend(info, padded, keys[None], values[None], None, True, False, "attend_own")
    for i, (kg, vg) in enumerate(gathered):
        final = i == len(gathered) - 1
        state = attend(info, padded, kg, vg, state, False, final, f"attend_{i}")
    attended = state[0]
    partial_value = lax.dot_general(
        attended, w_out, (((0,), (0,)), ((), ())), preferred_element_type=jnp.float32
    )
    summed = lax.psum_scatter(
        partial_value.astype(jnp.bfloat16), "heads", scatter_dimension=1, tiled=True
    ).astype(jnp.float32)
    return (tokens.astype(jnp.float32) + summed + out_bias).astype(jnp.bfloat16)


def solution(mesh):
    return jax.shard_map(
        functools.partial(per_device, (1, 1)),
        mesh=mesh,
        in_specs=(
            P(("rows", "cols"), "heads"),
            P(),
            P(None, None, "heads"),
            P("heads", None),
            P("heads"),
        ),
        out_specs=P(("rows", "cols"), "heads"),
        check_vma=False,
    )
```

time: 809 us -> 759 us (0.938)
  Pallas kernels: 0 us -> 532 us
  matrix products: 231 us -> 13.1 us
  local copies, waits for them, and re-layouts: 194 us -> 12.8 us
  other arithmetic: 121 us -> 6.99 us
  waiting for transfers between devices: 242 us -> 145 us
  blocking collectives: 0 us -> 34.7 us
    pallas_call x0 -> x3, Pallas kernels: none -> 532 us  [attend(): pl.pallas_call(functools.partial(attend_kernel, first, last), grid_spec=p...]
    dot_general x66 -> x6, matrix products: 231 us -> 13.1 us  [the longest x1 3.23 us: per_device(): jnp.dot(normed, w_qkv[1], preferred_element_type=jnp.float32)]
    reduce_sum x32 -> x0, other arithmetic: 110 us -> none  [one_block(): total = total * factor + jnp.sum(weights, axis=-1)]
    all_gather x2 -> x4, waiting for transfers between devices: 173 us -> 75.2 us  [the longest x2 74.9 us: per_device(): vg = lax.all_gather(values[:, lo:hi], both, axis=0)]
    reshape x2 -> x0, local copies, waits for them, and re-layouts: 82.7 us -> none  [the longest x1 41.4 us: per_device(): kblocks = keys.reshape(count // kblock, kblock, local_heads, head_dim)]
    while x259 -> x0, local copies, waits for them, and re-layouts: 73.4 us -> none  [the longest x3 72.7 us: per_device(): result, unused = lax.scan(step, initial, (kblocks, vblocks))]
    pmax x0 -> x1, blocking collectives: none -> 34.7 us  [per_device(): knorm = lax.pmax(knorm, both)]
    squeeze x16 -> x0, local copies, waits for them, and re-layouts: 28.4 us -> none  [per_device(): result, unused = lax.scan(step, initial, (kblocks, vblocks))]
  transfers between devices with their start and end apart: 4 -> 6, of which waited for: 4 -> 4; matrix products, arithmetic and copies ran while one was open for 10% -> 1% of each run, Pallas kernels for 0% -> 37%
where the time goes in v1:
time: 759 us
  Pallas kernels  532 us (70%)
  waiting for transfers between devices  145 us (19%)
  blocking collectives  34.7 us (5%)
  between operations  14.3 us (2%)
  matrix products  13.1 us (2%)
  local copies, waits for them, and re-layouts  12.8 us (2%)
    pallas_call x3, Pallas kernels, attend(): pl.pallas_call(functools.partial(attend_kernel, first, last), grid_spec=p...  532 us
    all_gather x2, waiting for transfers between devices, per_device(): vg = lax.all_gather(values[:, lo:hi], both, axis=0)  74.9 us
    all_gather x1, waiting for transfers between devices, per_device(): whole = lax.all_gather(tokens, 'heads', axis=1, tiled=True)  37.4 us
    pmax x1, blocking collectives, per_device(): knorm = lax.pmax(knorm, both)  34.7 us
    reduce_scatter x1, waiting for transfers between devices, per_device(): lax.psum_scatter(partial_value.astype(jnp.bfloat16), 'heads', scatter_dim...  30.7 us
  transfers between devices with their start and end apart: 6, of which 4 were waited for; matrix products, arithmetic and copies ran while one was open for 1% of the time, Pallas kernels for 37%

profile of v1, /device:TPU:0, one launch (start us, length us, event | category | flops | bytes accessed | tf_op | source)
XLA Modules:
  0.0 758.8 jit_solution(17639282202492835835)
XLA Ops:
  6.5 0.0 all-gather.10.cloned.1.call-start
  6.5 0.7 all-gather.10.cloned.1.call-update
  7.3 0.0 all-gather.16.cloned.1.call-start
  7.3 37.4 %all-gather.10.cloned.1.call-done = bf16[1024,1024]{1,0:T(8,128)(2,1)} async-done(((bf16[1024,512]{1,0:T(8,128)(2,1)}), bf16[1024,1024]{1,0:T(8,128)(2,1)}) %all-gather.10.cloned.1.call-update) | async-done | bytes 2097168 | tf_op jit(solution)/shard_map/all_gather | solution.py:151
  44.7 2.1 convert_reduce_fusion
  46.8 0.1 copy-done.8
  46.9 0.7 fusion.2
  47.7 0.7 fusion.4
  48.3 0.0 copy-start.11
  48.4 3.2 convolution_convert_fusion.2
  51.6 1.1 fusion.14
  52.7 0.0 all-gather.16.cloned.1.call-update
  52.7 0.0 all-gather.18.cloned.1.call-start
  52.8 3.1 convolution_convert_fusion.1
  55.9 1.1 fusion.13
  57.0 0.0 all-gather.18.cloned.1.call-update
  57.0 0.0 all-gather.12.cloned.1.call-start
  57.1 0.5 all-gather.12.cloned.1.call-update
  57.6 0.0 all-gather.14.cloned.1.call-start
  57.7 0.5 all-gather.14.cloned.1.call-update
  58.2 0.0 reduce-scatter.2.cloned.1.call-start
  58.3 0.1 mul.66
  58.3 0.1 mul.67
  58.5 0.5 convolution_reduce_fusion.1
  59.0 34.7 %pmax.7 = f32[8]{0:T(128)S(1)} all-reduce(f32[8]{0:T(128)S(1)} %convolution_reduce_fusion.1), channel_id=1, replica_groups=mesh['rows'=4,'cols'=4,'heads'=2] {'rows','cols'}, use_global_device_ids=true, to_apply=%region_3.0 | all-reduce | flops 8 | bytes 64 | tf_op jit(solution)/shard_map/pmax | solution.py:186
  93.7 3.2 multiply_convert_fusion.1
  96.9 0.0 copy-start.9
  96.9 1.0 copy-done.9
  97.9 0.4 convolution_reduce_fusion
  98.3 0.7 compare_reduce_fusion
  99.7 0.1 pad_add_fusion.info_ref
  99.8 1.5 mul.64
  101.3 0.2 broadcast_multiply_fusion.q_ref
  101.5 25.2 %attend_own.1 = (f32[8,80,1024]{2,1,0:T(8,128)}, f32[8,8,1024]{2,1,0:T(8,128)S(1)}) custom-call(s32[2]{0:T(128)S(1)} %pad_add_fusion.info_ref, bf16[8,128,1024]{2,1,0:T(8,128)(2,1)S(1)} %broadcast_multiply_fusion.q_ref, bf16[1,1024,512]{2,1,0:T(8,128)(2,1)S(1)} %bitcast.35, bf16[1,512,1024]{2,1,0:T(8,128)(2,1)S(1)} %bitcast.37), custom_call_target="tpu_custom_call" | custom-call | flops 8589934592 | bytes 2097152 | tf_op jit(solution)/shard_map/attend_own/pallas_call | solution.py:130
  126.7 1.3 copy-done.1
  128.0 0.3 all-gather.16.cloned.1.call-done
  128.3 74.9 %all-gather.18.cloned.1.call-done = bf16[8192,512]{1,0:T(8,128)(2,1)} async-done(((bf16[512,512]{1,0:T(8,128)(2,1)}), bf16[8192,512]{1,0:T(8,128)(2,1)}) %all-gather.18.cloned.1.call-update) | async-done | bytes 8388624 | tf_op jit(solution)/shard_map/all_gather | solution.py:169
  203.2 1.6 copy-done.2
  204.8 252.6 %attend_0.1 = (f32[8,80,1024]{2,1,0:T(8,128)S(1)}, f32[8,8,1024]{2,1,0:T(8,128)S(1)}) custom-call(s32[2]{0:T(128)S(1)} %pad_add_fusion.info_ref, bf16[8,128,1024]{2,1,0:T(8,128)(2,1)S(1)} %copy-done.2, bf16[16,512,512]{2,1,0:T(8,128)(2,1)} %bitcast.42, bf16[16,512,512]{2,1,0:T(8,128)(2,1)} %bitcast.44, f32[8,80,1024]{2,1,0:T(8,128)} %get-tuple-element.9.rest_0_, ...), custom_call_target="tpu_custom_call" | custom-call | flops 64424509440 | bytes 15728640 | tf_op jit(solution)/shard_map/attend_0/pallas_call | solution.py:130
  457.5 1.5 copy-done.4
  459.0 0.7 copy-done.6
  459.7 1.7 copy-done.5
  461.4 0.9 copy-done.7
  462.4 253.8 %attend_1.1 = bf16[512,1024]{1,0:T(8,128)(2,1)S(1)} custom-call(s32[2]{0:T(128)S(1)} %pad_add_fusion.info_ref, bf16[8,128,1024]{2,1,0:T(8,128)(2,1)S(1)} %copy-done.3, bf16[16,512,512]{2,1,0:T(8,128)(2,1)} %bitcast.43, bf16[16,512,512]{2,1,0:T(8,128)(2,1)} %bitcast.45, f32[8,80,1024]{2,1,0:T(8,128)S(1)} %copy-done.5, f32[8,8,1024]{2,1,0:T(8,128)S(1)} %copy-done.7), custom_call_target="tpu_custom_call" | custom-call | flops 64424509440 | bytes 15728640 | tf_op jit(solution)/shard_map/attend_1/pallas_call | solution.py:130
  716.1 2.6 convolution_convert_fusion
  718.8 0.0 reduce-scatter.2.cloned.1.call-update
  718.8 30.7 %reduce-scatter.2.cloned.1.call-done = bf16[1024,512]{1,0:T(8,128)(2,1)} async-done(((bf16[1024,1024]{1,0:T(8,128)(2,1)}), bf16[1024,512]{1,0:T(8,128)(2,1)}) %reduce-scatter.2.cloned.1.call-update) | async-done | bytes 1048592 | tf_op jit(solution)/shard_map/reduce_scatter | solution.py:200
  749.5 2.5 add_convert_fusion
  (25 shorter events, 0.1 us)
Async XLA Ops:
  6.5 709.6 %copy-start = (bf16[512,1024]{1,0:T(8,128)(2,1)S(1)}, bf16[512,1024]{1,0:T(8,128)(2,1)}, u32[]{:S(2)}) copy-start(bf16[512,1024]{1,0:T(8,128)(2,1)} %param.8) | copy-start | bytes 3145732
  6.5 38.2 %all-gather.10.cloned.1.call-start = ((), (), s32[]{:S(2)}) async-start(), calls=%async_computation.1 | async-start | bytes 3145728 | tf_op jit(solution)/shard_map/all_gather | solution.py:151
  7.3 40.4 %copy-start.12 = (f32[1024]{0:T(1024)S(1)}, f32[1024]{0:T(1024)}, u32[]{:S(2)}) copy-start(f32[1024]{0:T(1024)} %param.6) | copy-start | bytes 12292
  7.3 121.0 %all-gather.16.cloned.1.call-start = ((), (), s32[]{:S(2)}) async-start(), calls=%async_computation.5 | async-start | bytes 8912896 | tf_op jit(solution)/shard_map/all_gather | solution.py:168
  44.7 2.2 copy-start.8
  48.3 3.2 copy-start.11
  52.7 150.5 %all-gather.18.cloned.1.call-start = ((), (), s32[]{:S(2)}) async-start(), calls=%async_computation.6 | async-start | bytes 8912896 | tf_op jit(solution)/shard_map/all_gather | solution.py:169
  57.0 402.6 %all-gather.12.cloned.1.call-start = ((), (), s32[]{:S(2)}) async-start(), calls=%async_computation.3 | async-start | bytes 8912896 | tf_op jit(solution)/shard_map/all_gather | solution.py:168
  57.6 402.0 %all-gather.14.cloned.1.call-start = ((), (), s32[]{:S(2)}) async-start(), calls=%async_computation.4 | async-start | bytes 8912896 | tf_op jit(solution)/shard_map/all_gather | solution.py:169
  58.2 691.3 %reduce-scatter.2.cloned.1.call-start = ((), (), s32[]{:S(2)}) async-start(), calls=%async_computation.2 | async-start | bytes 3145728 | tf_op jit(solution)/shard_map/reduce_scatter | solution.py:200
  96.9 1.0 copy-start.9
  126.7 1.4 copy-start.1
  203.2 1.6 copy-start.2
  204.8 254.8 %copy-start.3 = (bf16[8,128,1024]{2,1,0:T(8,128)(2,1)S(1)}, bf16[8,128,1024]{2,1,0:T(8,128)(2,1)}, u32[]{:S(2)}) copy-start(bf16[8,128,1024]{2,1,0:T(8,128)(2,1)} %copy-done.1) | copy-start | bytes 6291460
  457.5 1.5 copy-start.4
  458.9 0.7 copy-start.6
  459.7 1.7 copy-start.5
  461.4 0.9 copy-start.7
  718.8 30.7 %copy-start.10 = (bf16[1024,512]{1,0:T(8,128)(2,1)S(1)}, bf16[1024,512]{1,0:T(8,128)(2,1)}, u32[]{:S(2)}) copy-start(bf16[1024,512]{1,0:T(8,128)(2,1)} %param.5) | copy-start | bytes 3145732
  718.8 30.7 %copy-start.13 = (f32[512]{0:T(512)S(1)}, f32[512]{0:T(512)}, u32[]{:S(2)}) copy-start(f32[512]{0:T(512)} %param.9) | copy-start | bytes 6148
Sparse Core Ops, SparseCore 0:
  8.9 35.8 all-gather.9
  52.9 75.4 all-gather.15
  130.5 72.6 all-gather.17
  205.3 73.0 all-gather.11
  280.5 73.1 all-gather.13
  718.9 30.4 reduce-scatter.1
